TPU v7x, 32 devices: a whole 2x2x4 slice. The times are simulated.
32 devices in a mesh: groups: 2 (over y), gx: 4 (over z), gy: 2 (over x), gz: 2 (over core).
Axes of the slice: x: 2, y: 2, z: 4, core: 2. Of those that a mesh axis runs over, the one named last changes fastest.
Arguments:
- latents: bfloat16 [8, 2, 2, 128, 128], P(('groups', 'gx'), 'gy', 'gz'), parts along dimension 0, may hold values from -6 to 6
- offsets: bfloat16 [8, 2, 2, 3, 128], P(('groups', 'gx'), 'gy', 'gz'), parts along dimension 0, may hold values from 0 to 1
- neighbours: int32 [8, 2, 2, 384], P(('groups', 'gx'), 'gy', 'gz'), parts along dimension 0, may hold values from 0 to 2047, as said below
- counts: int32 [8, 2, 2], P(('groups', 'gx'), 'gy', 'gz'), parts along dimension 0, may hold values from 1 to 384, as said below
- w_recv: bfloat16 [1, 128, 128], replicated, may hold values from -0.5 to 0.5
- w_send: bfloat16 [1, 128, 128], replicated, may hold values from -0.5 to 0.5
- w_rel: bfloat16 [1, 4, 128], replicated, may hold values from -3 to 3
- b_first: float32 [1, 128], replicated, may hold values from -5 to 5
- w_edge: bfloat16 [1, 128, 128], replicated, may hold values from -0.5 to 0.5
- b_edge: float32 [1, 128], replicated, may hold values from -5 to 5
- w_self: bfloat16 [1, 128, 128], replicated, may hold values from -0.5 to 0.5
- w_agg: bfloat16 [1, 128, 128], replicated, may hold values from -0.5 to 0.5
- w_out: bfloat16 [1, 128, 128], replicated, may hold values from -0.5 to 0.5
- norm_gain: float32 [1, 128], replicated, may hold values from 0.1 to 1.9
Outputs:
- processed: bfloat16 [8, 2, 2, 128, 128], P(('groups', 'gx'), 'gy', 'gz'), parts along dimension 0
There are 2 independent parts, one for each index of `groups`. A program takes and returns all parts, laid end to end along the dimension named above; an argument that names none is the same for every part. Nothing has to cross between parts.
Inputs may be any that keep to these rules, and one draw needn't show every extreme that they name: `neighbours`: each sender is a particle of the same cell or of a cell whose three coordinates differ from the receiver cell's by at most one. Only the first counts[cell] senders of a cell are live, the rest is padding. In the cells whose first coordinate is below 1 all 384 senders are live.
All inputs are finite; a program needn't handle non-finite values.
Results may differ from a plain program's by a relative error of at most 0.0055.
Values may be sent and summed in bfloat16 or wider, within the bound.
A program may use at most 64 MiB of HBM per device.

v0:
```python
import jax
import jax.numpy as jnp
from jax import lax
from jax.sharding import PartitionSpec as P

SLOTS = 128


def extended(shard, sides, width):
    for axis, dim in sides:
        size, length = (lax.axis_size(axis), shard.shape[dim])
        up = [(i, (i + 1) % size) for i in range(size - 1)]
        down = [(j, i) for i, j in up]
        last = lax.slice_in_dim(shard, length - width, length, axis=dim)
        first = lax.slice_in_dim(shard, 0, width, axis=dim)
        before = lax.ppermute(last, axis, up)
        after = lax.ppermute(first, axis, down)
        shard = jnp.concatenate([before, shard, after], axis=dim)
    return shard


def edge_sum(recv_term, send_term, recv_place, send_place, live_mask, rel_weight, w_edge, b_edge):
    row_count, latent_width = recv_term.shape
    tile_rows = min(16, row_count)
    tile_count = row_count // tile_rows

    def tile_messages(operands):
        recv_tile, place_tile = operands
        relative = send_place[:, None, :] - place_tile[:, :, None]
        features = jnp.concatenate(
            [relative, 0.25 * jnp.sum(relative * relative, axis=0, keepdims=True)], axis=0
        )
        place_term = jnp.einsum(
            "cij,cw->ijw", features, rel_weight, precision=lax.Precision.HIGHEST
        )
        pre_act = recv_tile[:, None, :] + send_term[None, :, :] + place_term
        edge_act = jax.nn.silu(pre_act).astype(jnp.bfloat16)
        message = (
            jnp.dot(edge_act.reshape(-1, latent_width), w_edge, preferred_element_type=jnp.float32)
            + b_edge
        )
        message = jax.nn.silu(message).reshape(tile_rows, -1, latent_width)
        return jnp.einsum("ijw,j->iw", message, live_mask, precision=lax.Precision.HIGHEST)

    recv_tiles = recv_term.reshape(tile_count, tile_rows, latent_width)
    place_tiles = recv_place.reshape(3, tile_count, tile_rows).transpose(1, 0, 2)
    return lax.map(tile_messages, (recv_tiles, place_tiles)).reshape(row_count, latent_width)


def renew(latent, summed, w_self, w_agg, w_out, norm_gain):
    pooled = (summed / latent.shape[0]).astype(jnp.bfloat16)
    hidden = jax.nn.silu(
        jnp.dot(latent, w_self, preferred_element_type=jnp.float32)
        + jnp.dot(pooled, w_agg, preferred_element_type=jnp.float32)
    ).astype(jnp.bfloat16)
    result = jnp.dot(hidden, w_out, preferred_element_type=jnp.float32)
    center = jnp.mean(result, axis=-1, keepdims=True)
    spread = jnp.mean((result - center) ** 2, axis=-1, keepdims=True)
    normed = (result - center) * lax.rsqrt(spread + 1e-05) * norm_gain
    return (latent.astype(jnp.float32) + normed).astype(jnp.bfloat16)


def widen(field):
    collected = lax.all_gather(field, "gy", axis=1, tiled=True)
    collected = lax.all_gather(collected, "gz", axis=2, tiled=True)
    return extended(collected, (("gx", 0),), 1)


def shards(
    latents,
    offsets,
    neighbours,
    counts,
    w_recv,
    w_send,
    w_rel,
    b_first,
    w_edge,
    b_edge,
    w_self,
    w_agg,
    w_out,
    norm_gain,
):
    span_x, span_y, span_z = (latents.shape[0], latents.shape[1], latents.shape[2])
    latent_width = latents.shape[4]
    cell_count = span_x * span_y * span_z
    index_x = lax.axis_index("gx")
    index_y = lax.axis_index("gy")
    index_z = lax.axis_index("gz")
    whole_y = span_y * lax.axis_size("gy")
    whole_z = span_z * lax.axis_size("gz")
    base_x = index_x * span_x - 1
    ext_rows = (span_x + 2) * whole_y * whole_z * SLOTS
    cell_of = neighbours // SLOTS
    slot_of = neighbours % SLOTS
    coord_z = cell_of % whole_z
    coord_y = cell_of // whole_z % whole_y
    coord_x = cell_of // (whole_y * whole_z)
    local_ids = (
        (((coord_x - base_x) * whole_y + coord_y) * whole_z + coord_z) * SLOTS + slot_of
    ).reshape(cell_count, -1)
    sender_coords = (
        jnp.stack([coord_x, coord_y, coord_z], axis=-2)
        .astype(jnp.float32)
        .reshape(cell_count, 3, -1)
    )
    grid_x = (index_x * span_x + lax.iota(jnp.int32, span_x))[:, None, None]
    grid_y = (index_y * span_y + lax.iota(jnp.int32, span_y))[None, :, None]
    grid_z = (index_z * span_z + lax.iota(jnp.int32, span_z))[None, None, :]
    own_coords = jnp.stack([grid_x, grid_y, grid_z], axis=-1).astype(jnp.float32)
    own_places = (offsets.astype(jnp.float32) + own_coords[..., None]).reshape(cell_count, 3, SLOTS)
    rim_offsets = widen(offsets)
    offset_table = rim_offsets.transpose(3, 0, 1, 2, 4).reshape(3, ext_rows)
    count_rows = counts.reshape(cell_count)
    blocks_needed = (count_rows + SLOTS - 1) // SLOTS
    slot_ids = lax.iota(jnp.int32, SLOTS)
    current = latents.reshape(cell_count, SLOTS, latent_width)
    step_index = 0
    rimmed = widen(current.reshape(span_x, span_y, span_z, SLOTS, latent_width)).reshape(
        ext_rows, latent_width
    )
    rel_weight = w_rel[step_index].astype(jnp.float32)

    def senders(cell_index, block_index, rimmed=rimmed, step_index=step_index):
        sender_ids = lax.dynamic_slice_in_dim(local_ids[cell_index], block_index * SLOTS, SLOTS)
        gathered = jnp.take(rimmed, sender_ids, axis=0)
        send_term = jnp.dot(gathered, w_send[step_index], preferred_element_type=jnp.float32)
        send_place = jnp.take(offset_table, sender_ids, axis=1).astype(
            jnp.float32
        ) + lax.dynamic_slice_in_dim(sender_coords[cell_index], block_index * SLOTS, SLOTS, axis=1)
        live_mask = (block_index * SLOTS + slot_ids < count_rows[cell_index]).astype(jnp.float32)
        return (send_term, send_place, live_mask)

    def block_sum(
        cell_index,
        recv_term,
        first_block,
        last_block,
        step_index=step_index,
        rel_weight=rel_weight,
        senders=senders,
    ):

        def add_block(block_index, summed):
            send_term, send_place, live_mask = senders(cell_index, block_index)
            return summed + edge_sum(
                recv_term,
                send_term,
                own_places[cell_index],
                send_place,
                live_mask,
                rel_weight,
                w_edge[step_index],
                b_edge[step_index],
            )

        return lax.fori_loop(
            first_block, last_block, add_block, jnp.zeros((SLOTS, latent_width), jnp.float32)
        )

    recv_terms = (
        jnp.dot(
            current.reshape(-1, latent_width),
            w_recv[step_index],
            preferred_element_type=jnp.float32,
        )
        + b_first[step_index]
    ).reshape(cell_count, SLOTS, latent_width)
    sums = block_sum(0, recv_terms[0], 0, blocks_needed[0])
    current = jnp.stack(
        [
            renew(
                current[0],
                sums,
                w_self[step_index],
                w_agg[step_index],
                w_out[step_index],
                norm_gain[step_index],
            )
        ]
    )
    return current.reshape(span_x, span_y, span_z, SLOTS, latent_width)


def solution(mesh):
    in_specs = (
        P(("groups", "gx"), "gy", "gz", None, None),
        P(("groups", "gx"), "gy", "gz", None, None),
        P(("groups", "gx"), "gy", "gz", None),
        P(("groups", "gx"), "gy", "gz"),
        P(),
        P(),
        P(),
        P(),
        P(),
        P(),
        P(),
        P(),
        P(),
        P(),
    )
    out_specs = P(("groups", "gx"), "gy", "gz", None, None)
    return jax.shard_map(shards, mesh=mesh, in_specs=in_specs, out_specs=out_specs, check_vma=False)
```

profile of v0, /device:TPU:0, one launch (start us, length us, event | category | flops | bytes accessed | tf_op | source)
XLA Modules:
  0.0 117.5 jit_solution(15140709854701901017)
XLA Ops:
  0.0 5.9 %all_gather.14 = bf16[1,2,1,128,128]{4,3,2,0,1:T(8,128)(2,1)S(1)} all-gather(bf16[1,1,1,128,128]{4,3,2,0,1:T(8,128)(2,1)} %bitcast.142), channel_id=1, replica_groups=mesh['groups'=2,'gx'=4,'gy'=2,'gz'=2] {'gy'}, dimensions={1}, use_global_device_ids=true | all-gather | bytes 98304 | tf_op jit(solution)/shard_map/all_gather | solution.py:64
  5.9 2.0 %all_gather.15 = bf16[1,2,2,128,128]{4,3,2,1,0:T(8,128)(2,1)S(1)} all-gather(bf16[1,2,1,128,128]{4,3,2,1,0:T(8,128)(2,1)S(1)} %bitcast.144), channel_id=1, replica_groups=mesh['groups'=2,'gx'=4,'gy'=2,'gz'=2] {'gz'}, dimensions={2}, use_global_device_ids=true | all-gather | bytes 196608 | tf_op jit(solution)/shard_map/all_gather | solution.py:65
  7.9 4.1 %collective-permute-start.2 = (bf16[1,2,2,128,128]{4,3,2,1,0:T(8,128)(2,1)S(1)}, bf16[1,2,2,128,128]{4,3,2,1,0:T(8,128)(2,1)S(1)}, u32[]{:S(2)}, u32[]{:S(2)}) collective-permute-start(bf16[1,2,2,128,128]{4,3,2,1,0:T(8,128)(2,1)S(1)} %all_gather.15), channel_id=1, source_target_pairs={{0,4},{4,8},{8,12},{1,5},{5,9},{9,13},{2,6},{6,10},{10,14},{3,7},{... | collective-permute-start | bytes 393224 | tf_op jit(solution)/shard_map/ppermute | solution.py:16
  12.0 1.3 %collective-permute-start.3 = (bf16[1,2,2,128,128]{4,3,2,1,0:T(8,128)(2,1)S(1)}, bf16[1,2,2,128,128]{4,3,2,1,0:T(8,128)(2,1)S(1)}, u32[]{:S(2)}, u32[]{:S(2)}) collective-permute-start(bf16[1,2,2,128,128]{4,3,2,1,0:T(8,128)(2,1)S(1)} %all_gather.15), channel_id=1, source_target_pairs={{4,0},{8,4},{12,8},{5,1},{9,5},{13,9},{6,2},{10,6},{14,10},{7,3},{... | collective-permute-start | bytes 393224 | tf_op jit(solution)/shard_map/ppermute | solution.py:17
  13.4 4.2 %all_gather.12 = bf16[1,2,1,3,128]{4,3,2,0,1:T(4,128)(2,1)S(1)} all-gather(bf16[1,1,1,3,128]{4,3,2,0,1:T(4,128)(2,1)S(1)} %bitcast.147), channel_id=1, replica_groups=mesh['groups'=2,'gx'=4,'gy'=2,'gz'=2] {'gy'}, dimensions={1}, use_global_device_ids=true | all-gather | bytes 2304 | tf_op jit(solution)/shard_map/all_gather | solution.py:64
  17.6 1.8 %all_gather.13 = bf16[1,2,2,3,128]{4,3,2,0,1:T(4,128)(2,1)S(1)} all-gather(bf16[1,2,1,3,128]{4,3,2,0,1:T(4,128)(2,1)S(1)} %all_gather.12), channel_id=1, replica_groups=mesh['groups'=2,'gx'=4,'gy'=2,'gz'=2] {'gz'}, dimensions={2}, use_global_device_ids=true | all-gather | bytes 4608 | tf_op jit(solution)/shard_map/all_gather | solution.py:65
  19.4 4.5 %collective-permute-start = (bf16[1,2,2,3,128]{4,3,2,0,1:T(4,128)(2,1)S(1)}, bf16[1,2,2,3,128]{4,3,2,0,1:T(4,128)(2,1)S(1)}, u32[]{:S(2)}, u32[]{:S(2)}) collective-permute-start(bf16[1,2,2,3,128]{4,3,2,0,1:T(4,128)(2,1)S(1)} %all_gather.13), channel_id=1, source_target_pairs={{0,4},{4,8},{8,12},{1,5},{5,9},{9,13},{2,6},{6,10},{10,14},{3,7},{... | collective-permute-start | bytes 9224 | tf_op jit(solution)/shard_map/ppermute | solution.py:16
  23.9 1.3 %collective-permute-start.1 = (bf16[1,2,2,3,128]{4,3,2,0,1:T(4,128)(2,1)S(1)}, bf16[1,2,2,3,128]{4,3,2,0,1:T(4,128)(2,1)S(1)}, u32[]{:S(2)}, u32[]{:S(2)}) collective-permute-start(bf16[1,2,2,3,128]{4,3,2,0,1:T(4,128)(2,1)S(1)} %all_gather.13), channel_id=1, source_target_pairs={{4,0},{8,4},{12,8},{5,1},{9,5},{13,9},{6,2},{10,6},{14,10},{7,3},{... | collective-permute-start | bytes 9224 | tf_op jit(solution)/shard_map/ppermute | solution.py:17
  27.9 1.6 %collective-permute-done.1 = bf16[1,2,2,3,128]{4,3,2,0,1:T(4,128)(2,1)S(1)} collective-permute-done((bf16[1,2,2,3,128]{4,3,2,0,1:T(4,128)(2,1)S(1)}, bf16[1,2,2,3,128]{4,3,2,0,1:T(4,128)(2,1)S(1)}, u32[]{:S(2)}, u32[]{:S(2)}) %collective-permute-start.1) | collective-permute-done | bytes 3104 | tf_op jit(solution)/shard_map/ppermute | solution.py:17
  29.9 0.7 copy-done.1
  30.6 85.0 %while.23 = (s32[]{:T(128)}, f32[128,128]{1,0:T(8,128)S(1)}, s32[]{:T(128)}, f32[128,128]{1,0:T(8,128)S(1)}, f32[1,1,1,3,128]{4,3,2,1,0:T(4,128)S(1)}, /*index=5...) while((s32[]{:T(128)}, f32[128,128]{1,0:T(8,128)S(1)}, ...), condition=%wide.region_4.5_spmd.clone, body=%wide.region_0.4_spmd.clone.sunk | while | flops 90240648 | bytes 3800472 | solution.py:158
  30.6 0.7 gather_fusion.1
  31.6 0.7 gather_fusion
  32.5 0.7 compare_convert_fusion.2
  33.3 25.6 %while.24 = (s32[]{:T(128)}, f32[8,16,128]{2,1,0:T(8,128)S(1)}, f32[8,16,128]{2,1,0:T(8,128)S(1)}, f32[128,128]{1,0:T(8,128)S(1)}, f32[3,128]{1,0:T(4,128)S(1)},...) while((s32[]{:T(128)}, f32[8,16,128]{2,1,0:T(8,128)S(1)}, ...), condition=%wide.region_3.3_spmd, body=%wide.region_1.2_spmd.sunk | while | flops 86009856 | bytes 3381177 | solution.py:47
  33.5 1.8 %multiply_convert_fusion.8 = bf16[16,128,128]{2,1,0:T(8,128)(2,1)S(1)} fusion(f32[128,128]{1,0:T(8,128)S(1)} %get-tuple-element.507, f32[16,128]{1,0:T(8,128)S(1)} %dynamic-slice_bitcast_fusion.2, f32[1,16,128]{2,0,1:T(1,128)S(1)} %bitcast.138, f32[3,16,128]{2,0,1:T(4,128)S(1)} %get-tuple-element.481, f32[4,128]{1,0:T(4,128)S(1)} %get-tuple-element.510), kind=kOutput, calls=%fused_computation.6.clone.1 | convolution fusion | flops 14426112 | bytes 632832 | tf_op jit(solution)/shard_map/while/body/while/body/eval_jaxpr/cij,cw->ijw/dot_general | solution.py:33
  35.8 0.7 fusion.62
  36.7 1.8 %multiply_convert_fusion.8 = bf16[16,128,128]{2,1,0:T(8,128)(2,1)S(1)} fusion(f32[128,128]{1,0:T(8,128)S(1)} %get-tuple-element.507, f32[16,128]{1,0:T(8,128)S(1)} %dynamic-slice_bitcast_fusion.2, f32[1,16,128]{2,0,1:T(1,128)S(1)} %bitcast.138, f32[3,16,128]{2,0,1:T(4,128)S(1)} %get-tuple-element.481, f32[4,128]{1,0:T(4,128)S(1)} %get-tuple-element.510), kind=kOutput, calls=%fused_computation.6.clone.1 | convolution fusion | flops 14426112 | bytes 632832 | tf_op jit(solution)/shard_map/while/body/while/body/eval_jaxpr/cij,cw->ijw/dot_general | solution.py:33
  39.0 0.7 fusion.62
  39.9 1.8 %multiply_convert_fusion.8 = bf16[16,128,128]{2,1,0:T(8,128)(2,1)S(1)} fusion(f32[128,128]{1,0:T(8,128)S(1)} %get-tuple-element.507, f32[16,128]{1,0:T(8,128)S(1)} %dynamic-slice_bitcast_fusion.2, f32[1,16,128]{2,0,1:T(1,128)S(1)} %bitcast.138, f32[3,16,128]{2,0,1:T(4,128)S(1)} %get-tuple-element.481, f32[4,128]{1,0:T(4,128)S(1)} %get-tuple-element.510), kind=kOutput, calls=%fused_computation.6.clone.1 | convolution fusion | flops 14426112 | bytes 632832 | tf_op jit(solution)/shard_map/while/body/while/body/eval_jaxpr/cij,cw->ijw/dot_general | solution.py:33
  42.2 0.7 fusion.62
  43.1 1.8 %multiply_convert_fusion.8 = bf16[16,128,128]{2,1,0:T(8,128)(2,1)S(1)} fusion(f32[128,128]{1,0:T(8,128)S(1)} %get-tuple-element.507, f32[16,128]{1,0:T(8,128)S(1)} %dynamic-slice_bitcast_fusion.2, f32[1,16,128]{2,0,1:T(1,128)S(1)} %bitcast.138, f32[3,16,128]{2,0,1:T(4,128)S(1)} %get-tuple-element.481, f32[4,128]{1,0:T(4,128)S(1)} %get-tuple-element.510), kind=kOutput, calls=%fused_computation.6.clone.1 | convolution fusion | flops 14426112 | bytes 632832 | tf_op jit(solution)/shard_map/while/body/while/body/eval_jaxpr/cij,cw->ijw/dot_general | solution.py:33
  45.4 0.7 fusion.62
  46.3 1.8 %multiply_convert_fusion.8 = bf16[16,128,128]{2,1,0:T(8,128)(2,1)S(1)} fusion(f32[128,128]{1,0:T(8,128)S(1)} %get-tuple-element.507, f32[16,128]{1,0:T(8,128)S(1)} %dynamic-slice_bitcast_fusion.2, f32[1,16,128]{2,0,1:T(1,128)S(1)} %bitcast.138, f32[3,16,128]{2,0,1:T(4,128)S(1)} %get-tuple-element.481, f32[4,128]{1,0:T(4,128)S(1)} %get-tuple-element.510), kind=kOutput, calls=%fused_computation.6.clone.1 | convolution fusion | flops 14426112 | bytes 632832 | tf_op jit(solution)/shard_map/while/body/while/body/eval_jaxpr/cij,cw->ijw/dot_general | solution.py:33
  48.6 0.7 fusion.62
  49.5 1.8 %multiply_convert_fusion.8 = bf16[16,128,128]{2,1,0:T(8,128)(2,1)S(1)} fusion(f32[128,128]{1,0:T(8,128)S(1)} %get-tuple-element.507, f32[16,128]{1,0:T(8,128)S(1)} %dynamic-slice_bitcast_fusion.2, f32[1,16,128]{2,0,1:T(1,128)S(1)} %bitcast.138, f32[3,16,128]{2,0,1:T(4,128)S(1)} %get-tuple-element.481, f32[4,128]{1,0:T(4,128)S(1)} %get-tuple-element.510), kind=kOutput, calls=%fused_computation.6.clone.1 | convolution fusion | flops 14426112 | bytes 632832 | tf_op jit(solution)/shard_map/while/body/while/body/eval_jaxpr/cij,cw->ijw/dot_general | solution.py:33
  51.8 0.7 fusion.62
  52.7 1.8 %multiply_convert_fusion.8 = bf16[16,128,128]{2,1,0:T(8,128)(2,1)S(1)} fusion(f32[128,128]{1,0:T(8,128)S(1)} %get-tuple-element.507, f32[16,128]{1,0:T(8,128)S(1)} %dynamic-slice_bitcast_fusion.2, f32[1,16,128]{2,0,1:T(1,128)S(1)} %bitcast.138, f32[3,16,128]{2,0,1:T(4,128)S(1)} %get-tuple-element.481, f32[4,128]{1,0:T(4,128)S(1)} %get-tuple-element.510), kind=kOutput, calls=%fused_computation.6.clone.1 | convolution fusion | flops 14426112 | bytes 632832 | tf_op jit(solution)/shard_map/while/body/while/body/eval_jaxpr/cij,cw->ijw/dot_general | solution.py:33
  55.0 0.7 fusion.62
  55.9 1.8 %multiply_convert_fusion.8 = bf16[16,128,128]{2,1,0:T(8,128)(2,1)S(1)} fusion(f32[128,128]{1,0:T(8,128)S(1)} %get-tuple-element.507, f32[16,128]{1,0:T(8,128)S(1)} %dynamic-slice_bitcast_fusion.2, f32[1,16,128]{2,0,1:T(1,128)S(1)} %bitcast.138, f32[3,16,128]{2,0,1:T(4,128)S(1)} %get-tuple-element.481, f32[4,128]{1,0:T(4,128)S(1)} %get-tuple-element.510), kind=kOutput, calls=%fused_computation.6.clone.1 | convolution fusion | flops 14426112 | bytes 632832 | tf_op jit(solution)/shard_map/while/body/while/body/eval_jaxpr/cij,cw->ijw/dot_general | solution.py:33
  58.2 0.7 fusion.62
  58.9 0.7 gather_fusion.1
  60.0 0.7 gather_fusion
  60.9 0.7 compare_convert_fusion.2
  61.6 25.6 %while.24 = (s32[]{:T(128)}, f32[8,16,128]{2,1,0:T(8,128)S(1)}, f32[8,16,128]{2,1,0:T(8,128)S(1)}, f32[128,128]{1,0:T(8,128)S(1)}, f32[3,128]{1,0:T(4,128)S(1)},...) while((s32[]{:T(128)}, f32[8,16,128]{2,1,0:T(8,128)S(1)}, ...), condition=%wide.region_3.3_spmd, body=%wide.region_1.2_spmd.sunk | while | flops 86009856 | bytes 3381177 | solution.py:47
  61.9 1.8 %multiply_convert_fusion.8 = bf16[16,128,128]{2,1,0:T(8,128)(2,1)S(1)} fusion(f32[128,128]{1,0:T(8,128)S(1)} %get-tuple-element.507, f32[16,128]{1,0:T(8,128)S(1)} %dynamic-slice_bitcast_fusion.2, f32[1,16,128]{2,0,1:T(1,128)S(1)} %bitcast.138, f32[3,16,128]{2,0,1:T(4,128)S(1)} %get-tuple-element.481, f32[4,128]{1,0:T(4,128)S(1)} %get-tuple-element.510), kind=kOutput, calls=%fused_computation.6.clone.1 | convolution fusion | flops 14426112 | bytes 632832 | tf_op jit(solution)/shard_map/while/body/while/body/eval_jaxpr/cij,cw->ijw/dot_general | solution.py:33
  65.1 1.8 %multiply_convert_fusion.8 = bf16[16,128,128]{2,1,0:T(8,128)(2,1)S(1)} fusion(f32[128,128]{1,0:T(8,128)S(1)} %get-tuple-element.507, f32[16,128]{1,0:T(8,128)S(1)} %dynamic-slice_bitcast_fusion.2, f32[1,16,128]{2,0,1:T(1,128)S(1)} %bitcast.138, f32[3,16,128]{2,0,1:T(4,128)S(1)} %get-tuple-element.481, f32[4,128]{1,0:T(4,128)S(1)} %get-tuple-element.510), kind=kOutput, calls=%fused_computation.6.clone.1 | convolution fusion | flops 14426112 | bytes 632832 | tf_op jit(solution)/shard_map/while/body/while/body/eval_jaxpr/cij,cw->ijw/dot_general | solution.py:33
  67.3 0.7 fusion.62
  68.3 1.8 %multiply_convert_fusion.8 = bf16[16,128,128]{2,1,0:T(8,128)(2,1)S(1)} fusion(f32[128,128]{1,0:T(8,128)S(1)} %get-tuple-element.507, f32[16,128]{1,0:T(8,128)S(1)} %dynamic-slice_bitcast_fusion.2, f32[1,16,128]{2,0,1:T(1,128)S(1)} %bitcast.138, f32[3,16,128]{2,0,1:T(4,128)S(1)} %get-tuple-element.481, f32[4,128]{1,0:T(4,128)S(1)} %get-tuple-element.510), kind=kOutput, calls=%fused_computation.6.clone.1 | convolution fusion | flops 14426112 | bytes 632832 | tf_op jit(solution)/shard_map/while/body/while/body/eval_jaxpr/cij,cw->ijw/dot_general | solution.py:33
  70.6 0.7 fusion.62
  71.5 1.8 %multiply_convert_fusion.8 = bf16[16,128,128]{2,1,0:T(8,128)(2,1)S(1)} fusion(f32[128,128]{1,0:T(8,128)S(1)} %get-tuple-element.507, f32[16,128]{1,0:T(8,128)S(1)} %dynamic-slice_bitcast_fusion.2, f32[1,16,128]{2,0,1:T(1,128)S(1)} %bitcast.138, f32[3,16,128]{2,0,1:T(4,128)S(1)} %get-tuple-element.481, f32[4,128]{1,0:T(4,128)S(1)} %get-tuple-element.510), kind=kOutput, calls=%fused_computation.6.clone.1 | convolution fusion | flops 14426112 | bytes 632832 | tf_op jit(solution)/shard_map/while/body/while/body/eval_jaxpr/cij,cw->ijw/dot_general | solution.py:33
  73.8 0.7 fusion.62
  74.7 1.8 %multiply_convert_fusion.8 = bf16[16,128,128]{2,1,0:T(8,128)(2,1)S(1)} fusion(f32[128,128]{1,0:T(8,128)S(1)} %get-tuple-element.507, f32[16,128]{1,0:T(8,128)S(1)} %dynamic-slice_bitcast_fusion.2, f32[1,16,128]{2,0,1:T(1,128)S(1)} %bitcast.138, f32[3,16,128]{2,0,1:T(4,128)S(1)} %get-tuple-element.481, f32[4,128]{1,0:T(4,128)S(1)} %get-tuple-element.510), kind=kOutput, calls=%fused_computation.6.clone.1 | convolution fusion | flops 14426112 | bytes 632832 | tf_op jit(solution)/shard_map/while/body/while/body/eval_jaxpr/cij,cw->ijw/dot_general | solution.py:33
  77.0 0.7 fusion.62
  77.9 1.8 %multiply_convert_fusion.8 = bf16[16,128,128]{2,1,0:T(8,128)(2,1)S(1)} fusion(f32[128,128]{1,0:T(8,128)S(1)} %get-tuple-element.507, f32[16,128]{1,0:T(8,128)S(1)} %dynamic-slice_bitcast_fusion.2, f32[1,16,128]{2,0,1:T(1,128)S(1)} %bitcast.138, f32[3,16,128]{2,0,1:T(4,128)S(1)} %get-tuple-element.481, f32[4,128]{1,0:T(4,128)S(1)} %get-tuple-element.510), kind=kOutput, calls=%fused_computation.6.clone.1 | convolution fusion | flops 14426112 | bytes 632832 | tf_op jit(solution)/shard_map/while/body/while/body/eval_jaxpr/cij,cw->ijw/dot_general | solution.py:33
  80.2 0.7 fusion.62
  81.1 1.8 %multiply_convert_fusion.8 = bf16[16,128,128]{2,1,0:T(8,128)(2,1)S(1)} fusion(f32[128,128]{1,0:T(8,128)S(1)} %get-tuple-element.507, f32[16,128]{1,0:T(8,128)S(1)} %dynamic-slice_bitcast_fusion.2, f32[1,16,128]{2,0,1:T(1,128)S(1)} %bitcast.138, f32[3,16,128]{2,0,1:T(4,128)S(1)} %get-tuple-element.481, f32[4,128]{1,0:T(4,128)S(1)} %get-tuple-element.510), kind=kOutput, calls=%fused_computation.6.clone.1 | convolution fusion | flops 14426112 | bytes 632832 | tf_op jit(solution)/shard_map/while/body/while/body/eval_jaxpr/cij,cw->ijw/dot_general | solution.py:33
  83.4 0.7 fusion.62
  84.3 1.8 %multiply_convert_fusion.8 = bf16[16,128,128]{2,1,0:T(8,128)(2,1)S(1)} fusion(f32[128,128]{1,0:T(8,128)S(1)} %get-tuple-element.507, f32[16,128]{1,0:T(8,128)S(1)} %dynamic-slice_bitcast_fusion.2, f32[1,16,128]{2,0,1:T(1,128)S(1)} %bitcast.138, f32[3,16,128]{2,0,1:T(4,128)S(1)} %get-tuple-element.481, f32[4,128]{1,0:T(4,128)S(1)} %get-tuple-element.510), kind=kOutput, calls=%fused_computation.6.clone.1 | convolution fusion | flops 14426112 | bytes 632832 | tf_op jit(solution)/shard_map/while/body/while/body/eval_jaxpr/cij,cw->ijw/dot_general | solution.py:33
  86.6 0.7 fusion.62
  87.3 0.7 gather_fusion.1
  88.3 0.7 gather_fusion
  89.2 0.7 compare_convert_fusion.2
  90.0 25.6 %while.24 = (s32[]{:T(128)}, f32[8,16,128]{2,1,0:T(8,128)S(1)}, f32[8,16,128]{2,1,0:T(8,128)S(1)}, f32[128,128]{1,0:T(8,128)S(1)}, f32[3,128]{1,0:T(4,128)S(1)},...) while((s32[]{:T(128)}, f32[8,16,128]{2,1,0:T(8,128)S(1)}, ...), condition=%wide.region_3.3_spmd, body=%wide.region_1.2_spmd.sunk | while | flops 86009856 | bytes 3381177 | solution.py:47
  90.2 1.8 %multiply_convert_fusion.8 = bf16[16,128,128]{2,1,0:T(8,128)(2,1)S(1)} fusion(f32[128,128]{1,0:T(8,128)S(1)} %get-tuple-element.507, f32[16,128]{1,0:T(8,128)S(1)} %dynamic-slice_bitcast_fusion.2, f32[1,16,128]{2,0,1:T(1,128)S(1)} %bitcast.138, f32[3,16,128]{2,0,1:T(4,128)S(1)} %get-tuple-element.481, f32[4,128]{1,0:T(4,128)S(1)} %get-tuple-element.510), kind=kOutput, calls=%fused_computation.6.clone.1 | convolution fusion | flops 14426112 | bytes 632832 | tf_op jit(solution)/shard_map/while/body/while/body/eval_jaxpr/cij,cw->ijw/dot_general | solution.py:33
  93.4 1.8 %multiply_convert_fusion.8 = bf16[16,128,128]{2,1,0:T(8,128)(2,1)S(1)} fusion(f32[128,128]{1,0:T(8,128)S(1)} %get-tuple-element.507, f32[16,128]{1,0:T(8,128)S(1)} %dynamic-slice_bitcast_fusion.2, f32[1,16,128]{2,0,1:T(1,128)S(1)} %bitcast.138, f32[3,16,128]{2,0,1:T(4,128)S(1)} %get-tuple-element.481, f32[4,128]{1,0:T(4,128)S(1)} %get-tuple-element.510), kind=kOutput, calls=%fused_computation.6.clone.1 | convolution fusion | flops 14426112 | bytes 632832 | tf_op jit(solution)/shard_map/while/body/while/body/eval_jaxpr/cij,cw->ijw/dot_general | solution.py:33
  96.6 1.8 %multiply_convert_fusion.8 = bf16[16,128,128]{2,1,0:T(8,128)(2,1)S(1)} fusion(f32[128,128]{1,0:T(8,128)S(1)} %get-tuple-element.507, f32[16,128]{1,0:T(8,128)S(1)} %dynamic-slice_bitcast_fusion.2, f32[1,16,128]{2,0,1:T(1,128)S(1)} %bitcast.138, f32[3,16,128]{2,0,1:T(4,128)S(1)} %get-tuple-element.481, f32[4,128]{1,0:T(4,128)S(1)} %get-tuple-element.510), kind=kOutput, calls=%fused_computation.6.clone.1 | convolution fusion | flops 14426112 | bytes 632832 | tf_op jit(solution)/shard_map/while/body/while/body/eval_jaxpr/cij,cw->ijw/dot_general | solution.py:33
  99.8 1.8 %multiply_convert_fusion.8 = bf16[16,128,128]{2,1,0:T(8,128)(2,1)S(1)} fusion(f32[128,128]{1,0:T(8,128)S(1)} %get-tuple-element.507, f32[16,128]{1,0:T(8,128)S(1)} %dynamic-slice_bitcast_fusion.2, f32[1,16,128]{2,0,1:T(1,128)S(1)} %bitcast.138, f32[3,16,128]{2,0,1:T(4,128)S(1)} %get-tuple-element.481, f32[4,128]{1,0:T(4,128)S(1)} %get-tuple-element.510), kind=kOutput, calls=%fused_computation.6.clone.1 | convolution fusion | flops 14426112 | bytes 632832 | tf_op jit(solution)/shard_map/while/body/while/body/eval_jaxpr/cij,cw->ijw/dot_general | solution.py:33
  103.0 1.8 %multiply_convert_fusion.8 = bf16[16,128,128]{2,1,0:T(8,128)(2,1)S(1)} fusion(f32[128,128]{1,0:T(8,128)S(1)} %get-tuple-element.507, f32[16,128]{1,0:T(8,128)S(1)} %dynamic-slice_bitcast_fusion.2, f32[1,16,128]{2,0,1:T(1,128)S(1)} %bitcast.138, f32[3,16,128]{2,0,1:T(4,128)S(1)} %get-tuple-element.481, f32[4,128]{1,0:T(4,128)S(1)} %get-tuple-element.510), kind=kOutput, calls=%fused_computation.6.clone.1 | convolution fusion | flops 14426112 | bytes 632832 | tf_op jit(solution)/shard_map/while/body/while/body/eval_jaxpr/cij,cw->ijw/dot_general | solution.py:33
  106.2 1.8 %multiply_convert_fusion.8 = bf16[16,128,128]{2,1,0:T(8,128)(2,1)S(1)} fusion(f32[128,128]{1,0:T(8,128)S(1)} %get-tuple-element.507, f32[16,128]{1,0:T(8,128)S(1)} %dynamic-slice_bitcast_fusion.2, f32[1,16,128]{2,0,1:T(1,128)S(1)} %bitcast.138, f32[3,16,128]{2,0,1:T(4,128)S(1)} %get-tuple-element.481, f32[4,128]{1,0:T(4,128)S(1)} %get-tuple-element.510), kind=kOutput, calls=%fused_computation.6.clone.1 | convolution fusion | flops 14426112 | bytes 632832 | tf_op jit(solution)/shard_map/while/body/while/body/eval_jaxpr/cij,cw->ijw/dot_general | solution.py:33
  109.4 1.8 %multiply_convert_fusion.8 = bf16[16,128,128]{2,1,0:T(8,128)(2,1)S(1)} fusion(f32[128,128]{1,0:T(8,128)S(1)} %get-tuple-element.507, f32[16,128]{1,0:T(8,128)S(1)} %dynamic-slice_bitcast_fusion.2, f32[1,16,128]{2,0,1:T(1,128)S(1)} %bitcast.138, f32[3,16,128]{2,0,1:T(4,128)S(1)} %get-tuple-element.481, f32[4,128]{1,0:T(4,128)S(1)} %get-tuple-element.510), kind=kOutput, calls=%fused_computation.6.clone.1 | convolution fusion | flops 14426112 | bytes 632832 | tf_op jit(solution)/shard_map/while/body/while/body/eval_jaxpr/cij,cw->ijw/dot_general | solution.py:33
  112.6 1.8 %multiply_convert_fusion.8 = bf16[16,128,128]{2,1,0:T(8,128)(2,1)S(1)} fusion(f32[128,128]{1,0:T(8,128)S(1)} %get-tuple-element.507, f32[16,128]{1,0:T(8,128)S(1)} %dynamic-slice_bitcast_fusion.2, f32[1,16,128]{2,0,1:T(1,128)S(1)} %bitcast.138, f32[3,16,128]{2,0,1:T(4,128)S(1)} %get-tuple-element.481, f32[4,128]{1,0:T(4,128)S(1)} %get-tuple-element.510), kind=kOutput, calls=%fused_computation.6.clone.1 | convolution fusion | flops 14426112 | bytes 632832 | tf_op jit(solution)/shard_map/while/body/while/body/eval_jaxpr/cij,cw->ijw/dot_general | solution.py:33
  116.0 0.7 copy-done.9
  116.7 0.7 copy.45
  (279 shorter events, 25.7 us)
Async XLA Ops:
  0.0 115.6 %copy-start = (bf16[1,128,128]{2,1,0:T(8,128)(2,1)S(1)}, bf16[1,128,128]{2,1,0:T(8,128)(2,1)}, u32[]{:S(2)}) copy-start(bf16[1,128,128]{2,1,0:T(8,128)(2,1)} %param.30) | copy-start | bytes 98308
  5.9 7.4 %copy-start.6 = (bf16[1,1,1,3,128]{4,3,2,1,0:T(4,128)(2,1)S(1)}, bf16[1,1,1,3,128]{4,3,2,1,0:T(4,128)(2,1)}, u32[]{:S(2)}) copy-start(bf16[1,1,1,3,128]{4,3,2,1,0:T(4,128)(2,1)} %param.19) | copy-start | bytes 2308
  5.9 19.3 %copy-start.5 = (s32[1,1,1,384]{3,2,1,0:T(1,128)S(1)}, s32[1,1,1,384]{3,2,1,0:T(1,128)}, u32[]{:S(2)}) copy-start(s32[1,1,1,384]{3,2,1,0:T(1,128)} %param.20) | copy-start | bytes 4612
  5.9 20.1 %copy-start.3 = (bf16[1,128,128]{2,1,0:T(8,128)(2,1)S(1)}, bf16[1,128,128]{2,1,0:T(8,128)(2,1)}, u32[]{:S(2)}) copy-start(bf16[1,128,128]{2,1,0:T(8,128)(2,1)} %param.28) | copy-start | bytes 98308
  7.9 18.1 %copy-start.2 = (bf16[1,1,1,128,128]{4,3,2,1,0:T(8,128)(2,1)S(1)}, bf16[1,1,1,128,128]{4,3,2,1,0:T(8,128)(2,1)}, u32[]{:S(2)}) copy-start(bf16[1,1,1,128,128]{4,3,2,1,0:T(8,128)(2,1)} %param.18) | copy-start | bytes 98308
  7.9 21.8 %collective-permute-start.2 = (bf16[1,2,2,128,128]{4,3,2,1,0:T(8,128)(2,1)S(1)}, bf16[1,2,2,128,128]{4,3,2,1,0:T(8,128)(2,1)S(1)}, u32[]{:S(2)}, u32[]{:S(2)}) collective-permute-start(bf16[1,2,2,128,128]{4,3,2,1,0:T(8,128)(2,1)S(1)} %all_gather.15), channel_id=1, source_target_pairs={{0,4},{4,8},{8,12},{1,5},{5,9},{9,13},{2,6},{6,10},{10,14},{3,7},{... | collective-permute-start | bytes 393224 | tf_op jit(solution)/shard_map/ppermute | solution.py:16
  12.0 17.7 %collective-permute-start.3 = (bf16[1,2,2,128,128]{4,3,2,1,0:T(8,128)(2,1)S(1)}, bf16[1,2,2,128,128]{4,3,2,1,0:T(8,128)(2,1)S(1)}, u32[]{:S(2)}, u32[]{:S(2)}) collective-permute-start(bf16[1,2,2,128,128]{4,3,2,1,0:T(8,128)(2,1)S(1)} %all_gather.15), channel_id=1, source_target_pairs={{4,0},{8,4},{12,8},{5,1},{9,5},{13,9},{6,2},{10,6},{14,10},{7,3},{... | collective-permute-start | bytes 393224 | tf_op jit(solution)/shard_map/ppermute | solution.py:17
  19.4 8.5 %collective-permute-start = (bf16[1,2,2,3,128]{4,3,2,0,1:T(4,128)(2,1)S(1)}, bf16[1,2,2,3,128]{4,3,2,0,1:T(4,128)(2,1)S(1)}, u32[]{:S(2)}, u32[]{:S(2)}) collective-permute-start(bf16[1,2,2,3,128]{4,3,2,0,1:T(4,128)(2,1)S(1)} %all_gather.13), channel_id=1, source_target_pairs={{0,4},{4,8},{8,12},{1,5},{5,9},{9,13},{2,6},{6,10},{10,14},{3,7},{... | collective-permute-start | bytes 9224 | tf_op jit(solution)/shard_map/ppermute | solution.py:16
  23.9 5.5 %collective-permute-start.1 = (bf16[1,2,2,3,128]{4,3,2,0,1:T(4,128)(2,1)S(1)}, bf16[1,2,2,3,128]{4,3,2,0,1:T(4,128)(2,1)S(1)}, u32[]{:S(2)}, u32[]{:S(2)}) collective-permute-start(bf16[1,2,2,3,128]{4,3,2,0,1:T(4,128)(2,1)S(1)} %all_gather.13), channel_id=1, source_target_pairs={{4,0},{8,4},{12,8},{5,1},{9,5},{13,9},{6,2},{10,6},{14,10},{7,3},{... | collective-permute-start | bytes 9224 | tf_op jit(solution)/shard_map/ppermute | solution.py:17
  25.4 0.7 copy-start.7
  26.1 0.8 copy-start.4
  26.2 0.7 copy-start.8
  29.8 0.8 copy-start.1
  29.8 0.8 copy-start.10
  29.8 0.8 copy-start.12
  30.6 85.0 %copy-start.11 = (bf16[1,128,128]{2,1,0:T(8,128)(2,1)S(1)}, bf16[1,128,128]{2,1,0:T(8,128)(2,1)}, u32[]{:S(2)}) copy-start(bf16[1,128,128]{2,1,0:T(8,128)(2,1)} %param.29) | copy-start | bytes 98308
  116.0 0.7 copy-start.9
where the time goes:
time: 118 us; the launch traced here: 117 us
  matrix products  71.3 us (60%)
  blocking collectives  14 us (12%)
  local copies, waits for them, and re-layouts  11.5 us (10%)
  starting transfers between devices  11.2 us (9%)
  other arithmetic  5.12 us (4%)
  loops' own time  1.81 us (2%)
  waiting for transfers between devices  1.59 us (1%)
    dot_general x24, matrix products, tile_messages(): jnp.einsum('cij,cw->ijw', features, rel_weight, precision=lax.Precision.H...  44.2 us
    dot_general x24, matrix products, tile_messages(): jnp.einsum('ijw,j->iw', message, live_mask, precision=lax.Precision.HIGHEST)  15.6 us
    dot_general x24, matrix products, tile_messages(): jnp.dot(edge_act.reshape(-1, latent_width), w_edge, preferred_element_typ...  10.3 us
    all_gather x2, blocking collectives, widen(): collected = lax.all_gather(field, 'gy', axis=1, tiled=True)  10.2 us
    ppermute x2, starting transfers between devices, extended(): before = lax.ppermute(last, axis, up)  8.62 us
    all_gather x2, blocking collectives, widen(): collected = lax.all_gather(collected, 'gz', axis=2, tiled=True)  3.82 us
    unnamed x28, local copies, waits for them, and re-layouts  3.08 us
    ppermute x2, starting transfers between devices, extended(): after = lax.ppermute(first, axis, down)  2.58 us
  transfers between devices with their start and end apart: 4, of which 1 were waited for; matrix products, arithmetic and copies ran while one was open for 1% of the time, Pallas kernels for 0%

commit v1 on v0

v1 whole, which is shorter than its diff:
```python
import functools

import jax
import jax.numpy as jnp
from jax import lax
from jax.experimental import pallas as pl
from jax.experimental.pallas import tpu as pltpu
from jax.sharding import PartitionSpec as P

MESH = pl.DeviceIdType.MESH
PACK = 16
GROUP = 16


def split(value, size):
    if size & (size - 1) == 0:
        return value >> (size.bit_length() - 1), value & (size - 1)
    return lax.div(value, size), lax.rem(value, size)


def wide(axis):
    return lax.axis_size(axis) > 2


def slots_of(axis):
    return min(lax.axis_size(axis), 3)


def moves(axis):
    size, here = lax.axis_size(axis), lax.axis_index(axis)
    if size == 1:
        return []
    if size == 2:
        return [(1 - here, None)]
    return [(here - 1, here > 0), (here + 1, here < size - 1)]


def slot_on(axis, source, target):
    return source - target + 1 if wide(axis) else source


def both(a, b):
    if a is None:
        return b
    return a if b is None else jnp.logical_and(a, b)


def guarded(condition, action):
    if condition is None:
        action()
    else:
        pl.when(condition)(action)


def kernel(
    counts_ref, latents_ref, offsets_ref, neighbours_ref, w_recv, w_send, w_rel, b_first, w_edge,
    b_edge, w_self, w_agg, w_out, norm_gain, out_ref, table, recv_half, send_half, scaled, pooled,
    pair_edge, send_sem, recv_sem, relay_sem,
):
    f32, bf16 = jnp.float32, jnp.bfloat16
    slots, width = latents_ref.shape[3], latents_ref.shape[4]
    senders = neighbours_ref.shape[3]
    blocks = senders // slots
    here = [lax.axis_index(axis) for axis in ("gx", "gy", "gz")]
    sizes = [lax.axis_size(axis) for axis in ("gx", "gy", "gz")]
    spans = [slots_of(axis) for axis in ("gx", "gy", "gz")]

    def slot(coords):
        return (coords[0] * spans[1] + coords[1]) * spans[2] + coords[2]

    own_coords = [slot_on(a, c, c) for a, c in zip(("gx", "gy", "gz"), here)]
    own = slot(own_coords)

    latent = latents_ref[0, 0, 0]
    place = offsets_ref[0, 0, 0].astype(f32)
    rows = lax.broadcasted_iota(jnp.int32, (PACK, slots), 0)
    extra = jnp.zeros((PACK, slots), f32)
    for c in range(3):
        extra = jnp.where(rows == c, place[c : c + 1, :], extra)
        extra = jnp.where(rows == 3 + c, here[c].astype(f32), extra)
    table[own, :slots, :] = latent
    table[own, slots:, :] = extra.astype(bf16)

    stay_x, stay_y = (here[0], None), (here[1], None)
    routes = []
    for x, when_x in [stay_x] + moves("gx"):
        for y, when_y in [stay_y] + moves("gy"):
            if x is here[0] and y is here[1]:
                continue
            routes.append((x, y, both(when_x, when_y)))
    routes.sort(key=lambda r: (r[0] is not here[0]) + (r[1] is not here[1]))
    has_mate = sizes[2] > 1
    mate = {"gz": 1 - here[2]}

    barrier = pltpu.get_barrier_semaphore()

    def hello(target):
        pl.semaphore_signal(barrier, inc=1, device_id=target, device_id_type=MESH)

    if has_mate:
        hello(mate)
    for x, y, when in routes:
        guarded(when, functools.partial(hello, {"gx": x, "gy": y}))
    peers = jnp.int32(1 if has_mate else 0)
    for x, y, when in routes:
        peers = peers + (1 if when is None else when.astype(jnp.int32))
    pl.semaphore_wait(barrier, peers)

    sends, relays = [], []
    for n, (x, y, when) in enumerate(routes):
        there = slot(
            [slot_on("gx", here[0], x), slot_on("gy", here[1], y), slot_on("gz", here[2], here[2])]
        )
        mine = slot(
            [slot_on("gx", x, here[0]), slot_on("gy", y, here[1]), slot_on("gz", here[2], here[2])]
        )
        copy = pltpu.make_async_remote_copy(
            src_ref=table.at[own],
            dst_ref=table.at[there],
            send_sem=send_sem.at[n],
            recv_sem=recv_sem.at[there],
            device_id={"gx": x, "gy": y},
            device_id_type=MESH,
        )
        arrival = pltpu.make_async_remote_copy(
            src_ref=table.at[own],
            dst_ref=table.at[mine],
            send_sem=send_sem.at[n],
            recv_sem=recv_sem.at[mine],
            device_id={"gx": x, "gy": y},
            device_id_type=MESH,
        )
        relay = pltpu.make_async_remote_copy(
            src_ref=table.at[mine],
            dst_ref=table.at[mine],
            send_sem=relay_sem.at[n],
            recv_sem=recv_sem.at[mine],
            device_id=mate,
            device_id_type=MESH,
        )
        mate_slot = slot(
            [slot_on("gx", x, here[0]), slot_on("gy", y, here[1]), 1 - here[2]]
        )
        mate_arrival = pltpu.make_async_remote_copy(
            src_ref=table.at[own],
            dst_ref=table.at[mate_slot],
            send_sem=relay_sem.at[n],
            recv_sem=recv_sem.at[mate_slot],
            device_id=mate,
            device_id_type=MESH,
        )
        sends.append((when, copy, arrival, mine))
        relays.append((relay, mate_arrival, mate_slot))
    last = len(routes)
    if has_mate:
        mate_own = slot([own_coords[0], own_coords[1], 1 - here[2]])
        mate_copy = pltpu.make_async_remote_copy(
            src_ref=table.at[own], dst_ref=table.at[own], send_sem=send_sem.at[last],
            recv_sem=recv_sem.at[own], device_id=mate, device_id_type=MESH,
        )
        mate_in = pltpu.make_async_remote_copy(
            src_ref=table.at[own], dst_ref=table.at[mate_own], send_sem=send_sem.at[last],
            recv_sem=recv_sem.at[mate_own], device_id=mate, device_id_type=MESH,
        )
    for when, copy, _, _ in sends:
        guarded(when, copy.start)
    if has_mate:
        mate_copy.start()

    def clear(which):
        table[which] = jnp.zeros(table.shape[1:], bf16)

    for (when, _, _, mine), (_, _, mate_slot) in zip(sends, relays):
        if when is not None:
            pl.when(jnp.logical_not(when))(functools.partial(clear, mine))
            if has_mate:
                pl.when(jnp.logical_not(when))(functools.partial(clear, mate_slot))

    cell, at = split(neighbours_ref[0, 0], slots)
    cell, z = split(cell, sizes[2])
    x, y = split(cell, sizes[1])
    found = [
        v - h + 1 if wide(a) else v for a, v, h in zip(("gx", "gy", "gz"), (x, y, z), here)
    ]
    row_ids = (slot(found) * slots + at).astype(f32)
    ids = jnp.concatenate(
        [
            jnp.broadcast_to(row_ids[:, b * slots : (b + 1) * slots], (slots, slots)).T
            for b in range(blocks)
        ],
        axis=0,
    ).astype(jnp.int32)
    lanes = lax.broadcasted_iota(jnp.int32, (senders, slots), 1)
    count = table.shape[0]
    chosen = jnp.concatenate(
        [jnp.where(ids - k * slots == lanes, 1.0, 0.0).astype(bf16) for k in range(count)], axis=1
    )

    rel = w_rel[0].astype(f32)
    place_cols = jnp.transpose(jnp.broadcast_to(place[:1], (slots, slots)))
    recv = jnp.dot(latent, w_recv[0], preferred_element_type=f32) + b_first[...]
    for c in range(3):
        if c:
            place_cols = jnp.transpose(jnp.broadcast_to(place[c : c + 1], (slots, slots)))
        recv = recv - place_cols * rel[c : c + 1]
    recv_half[...] = 0.5 * recv

    for (when, _, arrival, _), (relay, _, _) in zip(sends, relays):

        def pass_on(arrival=arrival, relay=relay):
            arrival.wait_recv()
            if has_mate:
                relay.start()

        guarded(when, pass_on)
    if has_mate:
        mate_in.wait_recv()
        for (when, _, _, _), (_, mate_arrival, _) in zip(sends, relays):
            guarded(when, mate_arrival.wait_recv)

    gathered = jnp.dot(
        chosen, table[:, :slots, :].reshape(count * slots, width), preferred_element_type=f32
    ).astype(bf16)
    feats = jnp.zeros((senders, PACK), f32)
    for k in range(count):
        feats = feats + lax.dot_general(
            chosen[:, k * slots : (k + 1) * slots],
            table[k, slots:, :],
            (((1,), (1,)), ((), ())),
            preferred_element_type=f32,
        )
    send = jnp.dot(gathered, w_send[0], preferred_element_type=f32)
    square = jnp.zeros((senders, slots), f32)
    for c in range(3):
        where = feats[:, c : c + 1] + (feats[:, 3 + c : 4 + c] - here[c].astype(f32))
        where = jnp.broadcast_to(where, (senders, slots))
        send = send + where * rel[c : c + 1]
        apart = where - place[c : c + 1]
        square = square + apart * apart
    send_half[...] = (0.5 * send).astype(bf16)
    scaled[...] = 0.25 * square

    rel_half = (0.5 * rel[3:4]).astype(bf16)
    edge_half = 0.5 * w_edge[0].astype(f32)
    nil = jnp.zeros_like(edge_half)
    pair_edge[...] = jnp.concatenate(
        [jnp.concatenate([edge_half, nil], axis=1), jnp.concatenate([nil, edge_half], axis=1)], axis=0
    ).astype(bf16)
    bias_half = (0.5 * b_edge[...]).astype(bf16)
    bias_pair = jnp.concatenate([bias_half, bias_half], axis=1)
    live = (
        lax.broadcasted_iota(jnp.int32, (8, senders), 1) < counts_ref[0]
    ).astype(f32).astype(bf16)

    @pl.loop(0, slots // GROUP)
    def _(group):
        base = pl.multiple_of(group * GROUP, GROUP)
        own_rows = recv_half[pl.ds(base, GROUP), :].astype(bf16)
        sums = []
        for i in range(0, GROUP, 2):
            total = jnp.zeros((8, 2 * width), f32)
            for b in range(blocks):
                span = slice(b * slots, (b + 1) * slots)
                halves = []
                for n in (i, i + 1):
                    s = jnp.broadcast_to(scaled[span, n : n + 1], (slots, width)).astype(bf16)
                    pre = own_rows[n : n + 1] + send_half[span, :] + s * rel_half
                    halves.append(pre * (jnp.tanh(pre) + 1))
                edge = jnp.concatenate(halves, axis=1)
                msg = jnp.dot(edge, pair_edge[...], preferred_element_type=f32).astype(bf16)
                msg = msg + bias_pair
                msg = msg * (jnp.tanh(msg) + 1)
                total = total + jnp.dot(live[:, span], msg, preferred_element_type=f32)
            sums += [total[:1, :width], total[:1, width:]]
        pooled[pl.ds(base, GROUP), :] = jnp.concatenate(sums, axis=0)
        scaled[...] = pltpu.roll(scaled[...], slots - GROUP, 1)

    mean = (pooled[...] / slots).astype(bf16)
    hidden = jax.nn.silu(
        jnp.dot(latent, w_self[0], preferred_element_type=f32)
        + jnp.dot(mean, w_agg[0], preferred_element_type=f32)
    ).astype(bf16)
    result = jnp.dot(hidden, w_out[0], preferred_element_type=f32)
    center = jnp.mean(result, axis=-1, keepdims=True)
    shifted = result - center
    spread = jnp.mean(shifted * shifted, axis=-1, keepdims=True)
    normed = shifted * lax.rsqrt(spread + 1e-05) * norm_gain[...]
    out_ref[0, 0, 0] = (latent.astype(f32) + normed).astype(bf16)

    for (when, copy, _, _), (relay, _, _) in zip(sends, relays):

        def finish(copy=copy, relay=relay):
            copy.wait_send()
            if has_mate:
                relay.wait_send()

        guarded(when, finish)
    if has_mate:
        mate_copy.wait_send()


def shards(latents, offsets, neighbours, counts, *weights):
    slots, width = latents.shape[3:]
    senders = neighbours.shape[3]
    count = slots_of("gx") * slots_of("gy") * slots_of("gz")
    routes = 9
    f32, bf16 = jnp.float32, jnp.bfloat16
    vmem = pl.BlockSpec(memory_space=pltpu.VMEM)
    return pl.pallas_call(
        kernel,
        out_shape=jax.ShapeDtypeStruct(latents.shape, latents.dtype),
        in_specs=[vmem] * (4 + len(weights)),
        out_specs=vmem,
        scratch_shapes=[
            pltpu.VMEM((count, slots + PACK, width), bf16),
            pltpu.VMEM((slots, width), f32),
            pltpu.VMEM((senders, width), bf16),
            pltpu.VMEM((senders, slots), f32),
            pltpu.VMEM((slots, width), f32),
            pltpu.VMEM((2 * width, 2 * width), bf16),
            pltpu.SemaphoreType.DMA((routes,)),
            pltpu.SemaphoreType.DMA((count,)),
            pltpu.SemaphoreType.DMA((routes,)),
        ],
        compiler_params=pltpu.CompilerParams(collective_id=0, has_side_effects=True),
    )(counts, latents, offsets, neighbours, *weights)


def solution(mesh):
    cells = ("groups", "gx"), "gy", "gz"
    in_specs = (P(*cells, None, None), P(*cells, None, None), P(*cells, None), P(*cells))
    in_specs += (P(),) * 10
    return jax.shard_map(
        shards, mesh=mesh, in_specs=in_specs, out_specs=P(*cells, None, None), check_vma=False
    )
```

time: 118 us -> 31 us (0.26)
  the two profiles are of different devices: /device:TPU:0 before, /device:TPU:1 now
where the time goes in v1:
time: 31 us; the launch traced here: 30.7 us
  Pallas kernels  28.7 us (93%)
  local copies, waits for them, and re-layouts  1.38 us (4%)
  between operations  0.66 us (2%)
    pallas_call x1, Pallas kernels, shards(): pl.pallas_call(kernel, out_shape=jax.ShapeDtypeStruct(latents.shape, late...  28.7 us
    unnamed x1, local copies, waits for them, and re-layouts  1.38 us

profile of v1, /device:TPU:1, one launch (start us, length us, event | category | flops | bytes accessed | tf_op | source)
XLA Modules:
  0.0 30.7 jit_solution(4178366850804385982)
XLA Ops:
  0.7 28.7 %shard_map.136 = bf16[1,1,1,128,128]{4,3,2,1,0:T(8,128)(2,1)} custom-call(s32[1,1,1]{2,1,0:T(1,128)S(6)} %copy.16.counts_ref, bf16[1,1,1,128,128]{4,3,2,1,0:T(8,128)(2,1)} %latents_ref.1, bf16[1,1,1,3,128]{4,3,2,1,0:T(4,128)(2,1)} %offsets_ref.1, s32[1,1,1,384]{3,2,1,0:T(1,128)} %neighbours_ref.1, bf16[1,128,128]{2,1,0:T(8,128)(2,1)} %w_recv.1, ...), custom_call_target="tpu_custom_call" | custom-call | tf_op jit(solution)/shard_map/pallas_call | solution.py:309
  29.3 1.4 %copy.17 = bf16[1,1,1,128,128]{4,3,2,1,0:T(8,128)(2,1)} copy(bf16[1,1,1,128,128]{4,3,2,1,0:T(8,128)(2,1)} %shard_map.136) | data formatting | bytes 65536

commit v2 on v1

--- a/solution.py
+++ b/solution.py
@@ -10,6 +10,9 @@
 MESH = pl.DeviceIdType.MESH
 PACK = 16
 GROUP = 16
+PAIRS = 1
+INPUTS = 14
+LOAD_ORDER = (1, 2, 3, 0) + tuple(range(4, 14))
 
 
 def split(value, size):
@@ -52,11 +55,19 @@
         pl.when(condition)(action)
 
 
-def kernel(
-    counts_ref, latents_ref, offsets_ref, neighbours_ref, w_recv, w_send, w_rel, b_first, w_edge,
-    b_edge, w_self, w_agg, w_out, norm_gain, out_ref, table, recv_half, send_half, scaled, pooled,
-    pair_edge, send_sem, recv_sem, relay_sem,
-):
+def kernel(*refs):
+    hbm, out_ref, held, scratch = refs[:INPUTS], refs[INPUTS], refs[INPUTS + 1 : 2 * INPUTS + 1], refs[2 * INPUTS + 1 :]
+    load_sem, table, recv_half, send_half, scaled, pooled, pair_edge, masked = scratch[:8]
+    send_sem, recv_sem, relay_sem = scratch[8:]
+    (
+        counts_ref, latents_ref, offsets_ref, neighbours_ref, w_recv, w_send, w_rel, b_first,
+        w_edge, b_edge, w_self, w_agg, w_out, norm_gain,
+    ) = held
+    loads = [
+        pltpu.make_async_copy(src, dst, load_sem.at[n]) for n, (src, dst) in enumerate(zip(hbm, held))
+    ]
+    for n in LOAD_ORDER:
+        loads[n].start()
     f32, bf16 = jnp.float32, jnp.bfloat16
     slots, width = latents_ref.shape[3], latents_ref.shape[4]
     senders = neighbours_ref.shape[3]
@@ -70,16 +81,6 @@
 
     own_coords = [slot_on(a, c, c) for a, c in zip(("gx", "gy", "gz"), here)]
     own = slot(own_coords)
-
-    latent = latents_ref[0, 0, 0]
-    place = offsets_ref[0, 0, 0].astype(f32)
-    rows = lax.broadcasted_iota(jnp.int32, (PACK, slots), 0)
-    extra = jnp.zeros((PACK, slots), f32)
-    for c in range(3):
-        extra = jnp.where(rows == c, place[c : c + 1, :], extra)
-        extra = jnp.where(rows == 3 + c, here[c].astype(f32), extra)
-    table[own, :slots, :] = latent
-    table[own, slots:, :] = extra.astype(bf16)
 
     stay_x, stay_y = (here[0], None), (here[1], None)
     routes = []
@@ -101,6 +102,18 @@
         hello(mate)
     for x, y, when in routes:
         guarded(when, functools.partial(hello, {"gx": x, "gy": y}))
+    for n in (1, 2):
+        loads[n].wait()
+    latent = latents_ref[0, 0, 0]
+    place = offsets_ref[0, 0, 0].astype(f32)
+    rows = lax.broadcasted_iota(jnp.int32, (PACK, slots), 0)
+    extra = jnp.zeros((PACK, slots), f32)
+    for c in range(3):
+        extra = jnp.where(rows == c, place[c : c + 1, :], extra)
+        extra = jnp.where(rows == 3 + c, here[c].astype(f32), extra)
+    table[own, :slots, :] = latent
+    table[own, slots:, :] = extra.astype(bf16)
+
     peers = jnp.int32(1 if has_mate else 0)
     for x, y, when in routes:
         peers = peers + (1 if when is None else when.astype(jnp.int32))
@@ -176,6 +189,9 @@
             if has_mate:
                 pl.when(jnp.logical_not(when))(functools.partial(clear, mate_slot))
 
+    loads[0].wait()
+    for n in range(3, INPUTS):
+        loads[n].wait()
     cell, at = split(neighbours_ref[0, 0], slots)
     cell, z = split(cell, sizes[2])
     x, y = split(cell, sizes[1])
@@ -238,7 +254,8 @@
         apart = where - place[c : c + 1]
         square = square + apart * apart
     send_half[...] = (0.5 * send).astype(bf16)
-    scaled[...] = 0.25 * square
+    square = 0.25 * square
+    scaled[...] = jnp.transpose(square)
 
     rel_half = (0.5 * rel[3:4]).astype(bf16)
     edge_half = 0.5 * w_edge[0].astype(f32)
@@ -246,34 +263,47 @@
     pair_edge[...] = jnp.concatenate(
         [jnp.concatenate([edge_half, nil], axis=1), jnp.concatenate([nil, edge_half], axis=1)], axis=0
     ).astype(bf16)
-    bias_half = (0.5 * b_edge[...]).astype(bf16)
-    bias_pair = jnp.concatenate([bias_half, bias_half], axis=1)
-    live = (
-        lax.broadcasted_iota(jnp.int32, (8, senders), 1) < counts_ref[0]
-    ).astype(f32).astype(bf16)
+    alive = lax.broadcasted_iota(jnp.int32, (senders, width), 0) < counts_ref[0]
+    masked[...] = jnp.where(alive, 0.5 * b_edge[...], -1e30).astype(bf16)
 
     @pl.loop(0, slots // GROUP)
     def _(group):
         base = pl.multiple_of(group * GROUP, GROUP)
         own_rows = recv_half[pl.ds(base, GROUP), :].astype(bf16)
+        near = scaled[pl.ds(base, GROUP), :].astype(bf16)
         sums = []
-        for i in range(0, GROUP, 2):
-            total = jnp.zeros((8, 2 * width), f32)
-            for b in range(blocks):
-                span = slice(b * slots, (b + 1) * slots)
+        for i in range(0, GROUP, 2 * PAIRS):
+            edges = []
+            for p in range(PAIRS):
                 halves = []
-                for n in (i, i + 1):
-                    s = jnp.broadcast_to(scaled[span, n : n + 1], (slots, width)).astype(bf16)
-                    pre = own_rows[n : n + 1] + send_half[span, :] + s * rel_half
+                for n in (i + 2 * p, i + 2 * p + 1):
+                    s = jnp.concatenate(
+                        [
+                            jnp.transpose(jnp.broadcast_to(near[n : n + 1, b : b + slots], (width, slots)))
+                            for b in range(0, senders, slots)
+                        ],
+                        axis=0,
+                    )
+                    pre = (own_rows[n : n + 1] + send_half[...]) + s * rel_half
                     halves.append(pre * (jnp.tanh(pre) + 1))
-                edge = jnp.concatenate(halves, axis=1)
-                msg = jnp.dot(edge, pair_edge[...], preferred_element_type=f32).astype(bf16)
-                msg = msg + bias_pair
+                edges.append(jnp.concatenate(halves, axis=1))
+            msgs = jnp.dot(
+                jnp.concatenate(edges, axis=0), pair_edge[...], preferred_element_type=f32
+            ).astype(bf16)
+            for n in range(2 * PAIRS):
+                p, h = divmod(n, 2)
+                msg = msgs[p * senders : (p + 1) * senders, h * width : (h + 1) * width]
+                msg = msg + masked[...]
                 msg = msg * (jnp.tanh(msg) + 1)
-                total = total + jnp.dot(live[:, span], msg, preferred_element_type=f32)
-            sums += [total[:1, :width], total[:1, width:]]
+                total = jnp.zeros((8, width), f32)
+                for b in range(0, senders, slots):
+                    parts = [msg[r : r + PACK] for r in range(b, b + slots, PACK)]
+                    while len(parts) > 1:
+                        parts = [v + w for v, w in zip(parts[::2], parts[1::2])]
+                    part = parts[0].astype(f32)
+                    total = total + (part[:8] + part[8:])
+                sums.append(jnp.sum(total, axis=0, keepdims=True))
         pooled[pl.ds(base, GROUP), :] = jnp.concatenate(sums, axis=0)
-        scaled[...] = pltpu.roll(scaled[...], slots - GROUP, 1)
 
     mean = (pooled[...] / slots).astype(bf16)
     hidden = jax.nn.silu(
@@ -306,24 +336,28 @@
     routes = 9
     f32, bf16 = jnp.float32, jnp.bfloat16
     vmem = pl.BlockSpec(memory_space=pltpu.VMEM)
+    args = (counts, latents, offsets, neighbours) + weights
     return pl.pallas_call(
         kernel,
         out_shape=jax.ShapeDtypeStruct(latents.shape, latents.dtype),
-        in_specs=[vmem] * (4 + len(weights)),
+        in_specs=[pl.BlockSpec(memory_space=pl.ANY)] * INPUTS,
         out_specs=vmem,
-        scratch_shapes=[
+        scratch_shapes=[pltpu.VMEM(a.shape, a.dtype) for a in args]
+        + [
+            pltpu.SemaphoreType.DMA((INPUTS,)),
             pltpu.VMEM((count, slots + PACK, width), bf16),
             pltpu.VMEM((slots, width), f32),
             pltpu.VMEM((senders, width), bf16),
-            pltpu.VMEM((senders, slots), f32),
+            pltpu.VMEM((slots, senders), f32),
             pltpu.VMEM((slots, width), f32),
             pltpu.VMEM((2 * width, 2 * width), bf16),
+            pltpu.VMEM((senders, width), bf16),
             pltpu.SemaphoreType.DMA((routes,)),
             pltpu.SemaphoreType.DMA((count,)),
             pltpu.SemaphoreType.DMA((routes,)),
         ],
         compiler_params=pltpu.CompilerParams(collective_id=0, has_side_effects=True),
-    )(counts, latents, offsets, neighbours, *weights)
+    )(*args)
 
 
 def solution(mesh):

time: 31 us -> 21.7 us (0.70)
  Pallas kernels: 28.7 us -> 19.4 us
    pallas_call x1, Pallas kernels: 28.7 us -> 19.4 us  [shards(): pl.pallas_call(kernel, out_shape=jax.ShapeDtypeStruct(latents.shape, late...]
where the time goes in v2:
time: 21.7 us; the launch traced here: 21.4 us
  Pallas kernels  19.4 us (89%)
  local copies, waits for them, and re-layouts  1.38 us (6%)
  between operations  0.66 us (3%)
    pallas_call x1, Pallas kernels, shards(): pl.pallas_call(kernel, out_shape=jax.ShapeDtypeStruct(latents.shape, late...  19.4 us
    unnamed x1, local copies, waits for them, and re-layouts  1.38 us

profile of v2, /device:TPU:1, one launch (start us, length us, event | category | flops | bytes accessed | tf_op | source)
XLA Modules:
  0.0 21.4 jit_solution(18123452881039393540)
XLA Ops:
  0.7 19.4 %shard_map.136 = bf16[1,1,1,128,128]{4,3,2,1,0:T(8,128)(2,1)} custom-call(s32[1,1,1]{2,1,0:T(1,128)S(6)} %copy.16.refs_0_, bf16[1,1,1,128,128]{4,3,2,1,0:T(8,128)(2,1)} %refs_1_.1, bf16[1,1,1,3,128]{4,3,2,1,0:T(4,128)(2,1)} %refs_2_.1, s32[1,1,1,384]{3,2,1,0:T(1,128)} %refs_3_.1, bf16[1,128,128]{2,1,0:T(8,128)(2,1)} %refs_4_.1, ...), custom_call_target="tpu_custom_call" | custom-call | tf_op jit(solution)/shard_map/pallas_call | solution.py:340
  20.1 1.4 %copy.17 = bf16[1,1,1,128,128]{4,3,2,1,0:T(8,128)(2,1)} copy(bf16[1,1,1,128,128]{4,3,2,1,0:T(8,128)(2,1)} %shard_map.136) | data formatting | bytes 65536

commit v3 on v2

--- a/solution.py
+++ b/solution.py
@@ -9,7 +9,7 @@
 
 MESH = pl.DeviceIdType.MESH
 PACK = 16
-GROUP = 16
+GROUP = 32
 PAIRS = 1
 INPUTS = 14
 LOAD_ORDER = (1, 2, 3, 0) + tuple(range(4, 14))
@@ -57,8 +57,8 @@
 
 def kernel(*refs):
     hbm, out_ref, held, scratch = refs[:INPUTS], refs[INPUTS], refs[INPUTS + 1 : 2 * INPUTS + 1], refs[2 * INPUTS + 1 :]
-    load_sem, table, recv_half, send_half, scaled, pooled, pair_edge, masked = scratch[:8]
-    send_sem, recv_sem, relay_sem = scratch[8:]
+    load_sem, table, recv_half, send_half, scaled, pooled, pair_edge, masked, chosen = scratch[:9]
+    send_sem, recv_sem, relay_sem = scratch[9:]
     (
         counts_ref, latents_ref, offsets_ref, neighbours_ref, w_recv, w_send, w_rel, b_first,
         w_edge, b_edge, w_self, w_agg, w_out, norm_gain,
@@ -208,9 +208,11 @@
     ).astype(jnp.int32)
     lanes = lax.broadcasted_iota(jnp.int32, (senders, slots), 1)
     count = table.shape[0]
-    chosen = jnp.concatenate(
-        [jnp.where(ids - k * slots == lanes, 1.0, 0.0).astype(bf16) for k in range(count)], axis=1
-    )
+    span_z = spans[2]
+    for k in range(count):
+        chosen[k // span_z, :, (k % span_z) * slots : (k % span_z + 1) * slots] = jnp.where(
+            ids - k * slots == lanes, 1.0, 0.0
+        ).astype(bf16)
 
     rel = w_rel[0].astype(f32)
     place_cols = jnp.transpose(jnp.broadcast_to(place[:1], (slots, slots)))
@@ -221,6 +223,19 @@
         recv = recv - place_cols * rel[c : c + 1]
     recv_half[...] = 0.5 * recv
 
+    def gather(line, carry):
+        picks, cells = chosen[line], table.at[pl.ds(line * span_z, span_z)]
+        found = jnp.dot(
+            picks, cells[:, :slots, :].reshape(span_z * slots, width), preferred_element_type=f32
+        )
+        marks = cells[:, slots:, :]
+        marks = jnp.concatenate([marks[k] for k in range(span_z)], axis=1)
+        feats = lax.dot_general(picks, marks, (((1,), (1,)), ((), ())), preferred_element_type=f32)
+        return (found, feats) if carry is None else (carry[0] + found, carry[1] + feats)
+
+    if has_mate:
+        mate_in.wait_recv()
+    carry = gather(slot([own_coords[0], own_coords[1], 0]) // span_z, None)
     for (when, _, arrival, _), (relay, _, _) in zip(sends, relays):
 
         def pass_on(arrival=arrival, relay=relay):
@@ -229,22 +244,11 @@
                 relay.start()
 
         guarded(when, pass_on)
-    if has_mate:
-        mate_in.wait_recv()
-        for (when, _, _, _), (_, mate_arrival, _) in zip(sends, relays):
+    for (when, _, _, mine), (_, mate_arrival, _) in zip(sends, relays):
+        if has_mate:
             guarded(when, mate_arrival.wait_recv)
-
-    gathered = jnp.dot(
-        chosen, table[:, :slots, :].reshape(count * slots, width), preferred_element_type=f32
-    ).astype(bf16)
-    feats = jnp.zeros((senders, PACK), f32)
-    for k in range(count):
-        feats = feats + lax.dot_general(
-            chosen[:, k * slots : (k + 1) * slots],
-            table[k, slots:, :],
-            (((1,), (1,)), ((), ())),
-            preferred_element_type=f32,
-        )
+        carry = gather(mine // span_z, carry)
+    gathered, feats = carry[0].astype(bf16), carry[1]
     send = jnp.dot(gathered, w_send[0], preferred_element_type=f32)
     square = jnp.zeros((senders, slots), f32)
     for c in range(3):
@@ -352,6 +356,7 @@
             pltpu.VMEM((slots, width), f32),
             pltpu.VMEM((2 * width, 2 * width), bf16),
             pltpu.VMEM((senders, width), bf16),
+            pltpu.VMEM((count // slots_of("gz"), senders, slots * slots_of("gz")), bf16),
             pltpu.SemaphoreType.DMA((routes,)),
             pltpu.SemaphoreType.DMA((count,)),
             pltpu.SemaphoreType.DMA((routes,)),

time: 21.7 us -> 21.1 us (0.972)
  Pallas kernels: 19.4 us -> 18.8 us
    pallas_call x1, Pallas kernels: 19.4 us -> 18.8 us  [shards(): pl.pallas_call(kernel, out_shape=jax.ShapeDtypeStruct(latents.shape, late...]
where the time goes in v3:
time: 21.1 us; the launch traced here: 20.8 us
  Pallas kernels  18.8 us (89%)
  local copies, waits for them, and re-layouts  1.38 us (7%)
  between operations  0.66 us (3%)
    pallas_call x1, Pallas kernels, shards(): pl.pallas_call(kernel, out_shape=jax.ShapeDtypeStruct(latents.shape, late...  18.8 us
    unnamed x1, local copies, waits for them, and re-layouts  1.38 us

profile of v3, /device:TPU:1, one launch (start us, length us, event | category | flops | bytes accessed | tf_op | source)
XLA Modules:
  0.0 20.8 jit_solution(9427633156781216070)
XLA Ops:
  0.7 18.8 %shard_map.136 = bf16[1,1,1,128,128]{4,3,2,1,0:T(8,128)(2,1)} custom-call(s32[1,1,1]{2,1,0:T(1,128)S(6)} %copy.16.refs_0_, bf16[1,1,1,128,128]{4,3,2,1,0:T(8,128)(2,1)} %refs_1_.1, bf16[1,1,1,3,128]{4,3,2,1,0:T(4,128)(2,1)} %refs_2_.1, s32[1,1,1,384]{3,2,1,0:T(1,128)} %refs_3_.1, bf16[1,128,128]{2,1,0:T(8,128)(2,1)} %refs_4_.1, ...), custom_call_target="tpu_custom_call" | custom-call | tf_op jit(solution)/shard_map/pallas_call | solution.py:344
  19.5 1.4 %copy.17 = bf16[1,1,1,128,128]{4,3,2,1,0:T(8,128)(2,1)} copy(bf16[1,1,1,128,128]{4,3,2,1,0:T(8,128)(2,1)} %shard_map.136) | data formatting | bytes 65536
